TPU v7x, 32 devices: a whole 2x2x4 slice. The times are simulated.
32 devices in a mesh: tm: 2 (over y), space: 4 (over z), member: 4 (over x, core).
Axes of the slice: x: 2, y: 2, z: 4, core: 2. Of those that a mesh axis runs over, the one named last changes fastest.
Arguments:
- obs_anom: bfloat16 [6, 2, 8, 256, 1024], P('tm', None, 'space', 'member'), may hold values from -0.59375 to 0.59375
- obs_prec: bfloat16 [6, 2, 8, 1024], P('tm', None, 'space'), may hold values from 0.29882812 to 3
- innov: bfloat16 [6, 2, 8, 1024], P('tm', None, 'space'), may hold values from -6 to 6
- obs_column: int32 [6, 2, 8, 1024], P('tm', None, 'space'), may hold values from 0 to 127
- cutoff: int32 [2, 8], replicated, may hold values from 1 to 2
- inv_root: float32 [2, 8, 256, 256], P('tm', 'space'), may hold values from -0.12 to 0.12
- state_anom: bfloat16 [2, 8, 256, 32, 128], P('tm', 'space', None, 'member'), may hold values from -6 to 6
- state_mean: float32 [2, 8, 32, 128], P('tm', 'space', 'member'), may hold values from -6 to 6
Outputs:
- analysis: bfloat16 [2, 8, 256, 32, 128], P('tm', 'space', None, 'member')
All inputs are finite; a program needn't handle non-finite values.
Results may differ from a plain program's by a relative error of at most 0.0062.
Values may be sent and summed in bfloat16 or wider, within the bound.
A program may use at most 64 MiB of HBM per device.

v0:
```python
import math
import jax
import jax.numpy as jnp
from jax import lax
from jax.sharding import PartitionSpec as P

K = 256
HALO = 2
NEWTON = 2


def with_halo(cells, sides, width):
    for axis, dim in sides:
        count = lax.axis_size(axis)
        head = lax.slice_in_dim(cells, 0, width, axis=dim)
        tail = lax.slice_in_dim(cells, cells.shape[dim] - width, cells.shape[dim], axis=dim)
        cells = jnp.concatenate(
            [
                lax.ppermute(tail, axis, [(i, (i + 1) % count) for i in range(count)]),
                cells,
                lax.ppermute(head, axis, [((i + 1) % count, i) for i in range(count)]),
            ],
            axis=dim,
        )
    return cells


def taper_weight(distance, reach_now, columns):
    scaled_reach = (reach_now + 0.5) * columns
    relative = distance / scaled_reach
    return jnp.square(jnp.maximum(1.0 - relative * relative, 0.0))


def tile_cutoffs(cutoff, first_tile, how_many):
    flattened = cutoff.reshape(-1)
    cycle_size = flattened.shape[0]
    wanted = (first_tile + jnp.arange(how_many, dtype=jnp.int32) + cycle_size) % cycle_size
    matches = wanted[:, None] == jnp.arange(cycle_size, dtype=jnp.int32)[None, :]
    return jnp.sum(jnp.where(matches, flattened[None, :], 0), axis=1).astype(jnp.float32)


def spread_sums(relaid, reaches, shifts, columns):
    members = relaid.shape[2] - 3
    tile_count = relaid.shape[1]
    window_len = shifts.shape[0]
    extended = tile_count + window_len - 1
    start_gram = jnp.zeros((extended, members, members), jnp.float32)
    start_proj = jnp.zeros((extended, members), jnp.float32)

    def add_tile(tile_index, carry):
        gram_sums, proj_sums = carry
        obs_slab = lax.dynamic_index_in_dim(relaid, tile_index, 1, keepdims=False)
        anomaly = obs_slab[:, :members]
        precision = obs_slab[:, members].astype(jnp.float32)
        innovation = obs_slab[:, members + 1].astype(jnp.float32)
        placing = obs_slab[:, members + 2].astype(jnp.float32)
        reach_now = lax.dynamic_slice_in_dim(reaches, tile_index, window_len, 0)
        distance = shifts[:, None, None] * columns + placing[None]
        coeffs = taper_weight(distance, reach_now[:, None, None], columns) * precision[None]
        scaled = (anomaly[None] * coeffs[:, :, None, :]).astype(jnp.bfloat16)
        weighted = (coeffs * innovation[None]).astype(jnp.bfloat16)
        gram_part = jnp.einsum("wsko,slo->wkl", scaled, anomaly, preferred_element_type=jnp.float32)
        proj_part = jnp.einsum("sko,wso->wk", anomaly, weighted, preferred_element_type=jnp.float32)
        gram_sums = lax.dynamic_update_slice_in_dim(
            gram_sums,
            lax.dynamic_slice_in_dim(gram_sums, tile_index, window_len, 0) + gram_part,
            tile_index,
            0,
        )
        proj_sums = lax.dynamic_update_slice_in_dim(
            proj_sums,
            lax.dynamic_slice_in_dim(proj_sums, tile_index, window_len, 0) + proj_part,
            tile_index,
            0,
        )
        return (gram_sums, proj_sums)

    return lax.fori_loop(0, tile_count, add_tile, (start_gram, start_proj))


def body(obs_anom, obs_prec, innov, obs_column, cutoff, inv_root, state_anom, state_mean):
    columns = state_anom.shape[-1]
    placing = (obs_column.astype(jnp.float32) + (0.5 - columns / 2)).astype(jnp.bfloat16)
    obs_info = jnp.stack([obs_prec, innov, placing], axis=3)
    quarter = obs_anom.shape[4] // lax.axis_size("member")
    own_part = lax.dynamic_slice_in_dim(obs_info, lax.axis_index("member") * quarter, quarter, 4)
    ensemble = lax.all_to_all(obs_anom, "member", split_axis=4, concat_axis=3, tiled=True)
    combined = jnp.concatenate([ensemble, own_part], axis=3)
    relaid = lax.all_to_all(combined, "tm", split_axis=1, concat_axis=0, tiled=True)[:, 0]
    tile_count = relaid.shape[1]
    first_tile = (
        lax.axis_index("tm") * lax.axis_size("space") + lax.axis_index("space")
    ) * tile_count
    window_len = 2 * HALO + 1
    reaches = tile_cutoffs(cutoff, first_tile - HALO, tile_count + 2 * HALO)
    shifts = (HALO - jnp.arange(window_len, dtype=jnp.int32)).astype(jnp.float32)
    ext_gram, ext_proj = spread_sums(relaid, reaches, shifts, columns)
    stacked = jnp.concatenate([ext_gram, ext_proj[:, None, :]], axis=1)
    outgoing = jnp.concatenate([stacked[:HALO], stacked[tile_count + HALO :]], axis=0)
    arrived = with_halo(outgoing, ((("tm", "space"), 0),), HALO)
    owned = stacked[HALO : HALO + tile_count]
    owned = owned.at[:HALO].add(arrived[:HALO])
    owned = owned.at[tile_count - HALO :].add(arrived[3 * HALO :])
    gram_sums = owned[:, :K]
    proj_sums = owned[:, K]
    gram_sums, proj_sums = lax.psum((gram_sums, proj_sums), "member")
    highest = lax.Precision.HIGHEST
    identity = jnp.eye(K, dtype=jnp.float32)
    system = (K - 1.0) * identity + gram_sums
    inv_sqrt = inv_root[0]
    for newton_step in range(NEWTON):
        square = jnp.einsum("tij,tjk->tik", inv_sqrt, inv_sqrt, precision=highest)
        applied = jnp.einsum("tij,tjk->tik", system, square, precision=highest)
        inv_sqrt = 1.5 * inv_sqrt - 0.5 * jnp.einsum(
            "tij,tjk->tik", inv_sqrt, applied, precision=highest
        )
    inner_prod = jnp.einsum("tij,tj->ti", inv_sqrt, proj_sums, precision=highest)
    mean_weight = jnp.einsum("tij,tj->ti", inv_sqrt, inner_prod, precision=highest)
    weights = (mean_weight[:, :, None] + math.sqrt(K - 1) * inv_sqrt).astype(jnp.bfloat16)
    anomalies = state_anom[0].reshape(tile_count, K, -1)
    mean_rows = state_mean[0].reshape(tile_count, 1, -1)
    result = (
        jnp.einsum("tij,tiq->tjq", weights, anomalies, preferred_element_type=jnp.float32)
        + mean_rows
    )
    return result.astype(jnp.bfloat16).reshape(state_anom.shape)


def solution(mesh):
    in_specs = (
        P("tm", None, "space", "member", None),
        P("tm", None, "space", None),
        P("tm", None, "space", None),
        P("tm", None, "space", None),
        P(),
        P("tm", "space", None, None),
        P("tm", "space", None, "member", None),
        P("tm", "space", "member", None),
    )
    out_specs = P("tm", "space", None, "member", None)
    return jax.shard_map(body, mesh=mesh, in_specs=in_specs, out_specs=out_specs, check_vma=False)
```

profile of v0, /device:TPU:0, one launch (start us, length us, event | category | flops | bytes accessed | tf_op | source)
XLA Modules:
  0.0 166.9 jit_solution(3729697214545219223)
XLA Ops:
  6.5 7.3 %copy.73 = bf16[3,2,2,64,1024]{3,0,2,1,4:T(4,128)(2,1)} copy(bf16[3,2,2,64,1024]{4,3,2,1,0:T(8,128)(2,1)} %param.18) | data formatting | bytes 3145728 | tf_op args[0]
  13.9 5.5 %reshape.154 = bf16[4,2,98304]{2,1,0:T(2,128)(2,1)} reshape(bf16[1024,2,2,3,64]{4,3,2,1,0:T(4,128)(2,1)} %bitcast.100) | data formatting | bytes 3145728
  19.4 4.4 %all-to-all-start = ((bf16[4,2,98304]{2,1,0:T(2,128)(2,1)}), bf16[4,2,98304]{2,1,0:T(2,128)(2,1)S(1)}, u32[]{:S(2)}, u32[]{:S(2)}) async-start(bf16[4,2,98304]{2,1,0:T(2,128)(2,1)} %reshape.154), calls=%async_computation | async-start | bytes 3145728 | tf_op jit(solution)/shard_map/all_to_all | solution.py:87
  23.9 19.9 %all-to-all-done = bf16[4,2,98304]{2,1,0:T(2,128)(2,1)S(1)} async-done(((bf16[4,2,98304]{2,1,0:T(2,128)(2,1)}), bf16[4,2,98304]{2,1,0:T(2,128)(2,1)S(1)}, u32[]{:S(2)}, u32[]{:S(2)}) %all-to-all-start) | async-done | bytes 1572896 | tf_op jit(solution)/shard_map/all_to_all | solution.py:87
  43.8 3.8 %reshape.155 = bf16[1024,2,2,3,64]{4,3,2,1,0:T(4,128)(2,1)} reshape(bf16[4,2,98304]{2,1,0:T(2,128)(2,1)S(1)} %all-to-all-done) | data formatting | bytes 3145728
  47.6 9.8 %copy.74 = bf16[3,2,2,4,64,256]{5,2,4,3,0,1:T(2,128)(2,1)S(1)} copy(bf16[3,2,2,4,64,256]{4,0,2,1,5,3:T(4,128)(2,1)} %bitcast.99) | data formatting | bytes 3145728 | tf_op jit(solution)/shard_map/all_to_all | solution.py:87
  57.4 3.2 %pad_maximum_fusion = bf16[3,2,2,259,256]{4,2,3,0,1:T(2,128)(2,1)} fusion(bf16[3,2,2,3,256]{4,2,3,0,1:T(2,128)(2,1)S(1)} %fusion.35, bf16[3,2,2,256,256]{4,2,3,0,1:T(2,128)(2,1)S(1)} %bitcast.102), kind=kLoop, calls=%fused_computation.29 | loop fusion | flops 795648 | bytes 3182592 | tf_op jit(solution)/shard_map/concatenate | solution.py:88
  60.6 3.8 %all-to-all-start.1 = ((bf16[3,2,2,259,256]{4,2,3,0,1:T(2,128)(2,1)}), bf16[3,2,2,259,256]{4,2,3,0,1:T(2,128)(2,1)S(1)}, u32[]{:S(2)}, u32[]{:S(2)}) async-start(bf16[3,2,2,259,256]{4,2,3,0,1:T(2,128)(2,1)} %pad_maximum_fusion), calls=%async_computation.1 | async-start | bytes 3182592 | tf_op jit(solution)/shard_map/all_to_all | solution.py:89
  64.6 0.2 select_reduce_fusion
  64.8 19.6 %all-to-all-done.1 = bf16[3,2,2,259,256]{4,2,3,0,1:T(2,128)(2,1)S(1)} async-done(((bf16[3,2,2,259,256]{4,2,3,0,1:T(2,128)(2,1)}), bf16[3,2,2,259,256]{4,2,3,0,1:T(2,128)(2,1)S(1)}, u32[]{:S(2)}, u32[]{:S(2)}) %all-to-all-start.1) | async-done | bytes 1591328 | tf_op jit(solution)/shard_map/all_to_all | solution.py:89
  84.4 1.2 copy-done
  85.6 1.6 copy.78
  87.2 0.1 broadcast_in_dim.48
  87.3 4.5 %while.20 = (s32[]{:T(128)}, f32[6,256,256]{2,1,0:T(8,128)S(1)}, f32[6,256]{1,0:T(8,128)S(1)}, bf16[6,2,259,256]{3,2,0,1:T(8,128)(2,1)S(1)}, f32[6]{0:T(128)S(1)}, /*index=5*/s32[]{:T(128)}, s32[]{:T(128)}) while((s32[]{:T(128)}, f32[6,256,256]{2,1,0:T(8,128)S(1)}, f32[6,256]{1,0:T(8,128)S(1)}, ...), condition=%wide.region_2.3_spmd.clone, body=%wide.region_1.2_spmd.clone.sunk | while | flops 1015346944 | bytes 9977029 | solution.py:78
  87.5 0.1 convert_multiply_fusion.2
  87.5 0.1 multiply_multiply_fusion.3
  87.7 0.1 slice_convert_fusion.7
  87.8 1.4 fusion.60
  89.2 0.3 fusion.61
  89.8 0.1 multiply_multiply_fusion.3
  89.9 0.1 slice_convert_fusion.7
  90.1 1.4 fusion.60
  91.4 0.3 fusion.61
  91.9 0.1 constant_dynamic-update-slice_fusion
  92.1 0.1 fusion.42
  92.2 0.3 copy.79
  92.5 1.8 %collective-permute-start = (f32[2,257,256]{2,0,1:T(2,128)S(1)}, f32[2,257,256]{2,0,1:T(2,128)S(1)}, u32[]{:S(2)}, u32[]{:S(2)}) collective-permute-start(f32[2,257,256]{2,0,1:T(2,128)S(1)} %copy.79), channel_id=1, source_target_pairs={{0,4},{4,8},{8,12},{12,16},{16,20},{20,24},{24,28},{28,0},{1,5},{5... | collective-permute-start | bytes 1579016 | tf_op jit(solution)/shard_map/ppermute | solution.py:19
  94.3 0.3 copy.81
  94.6 3.0 %collective-permute-start.1 = (f32[2,257,256]{2,0,1:T(2,128)S(1)}, f32[2,257,256]{2,0,1:T(2,128)S(1)}, u32[]{:S(2)}, u32[]{:S(2)}) collective-permute-start(f32[2,257,256]{2,0,1:T(2,128)S(1)} %copy.81), channel_id=1, source_target_pairs={{4,0},{8,4},{12,8},{16,12},{20,16},{24,20},{28,24},{0,28},{5,1},{9... | collective-permute-start | bytes 1579016 | tf_op jit(solution)/shard_map/ppermute | solution.py:21
  97.6 12.5 %collective-permute-done = f32[2,257,256]{2,0,1:T(2,128)S(1)} collective-permute-done((f32[2,257,256]{2,0,1:T(2,128)S(1)}, f32[2,257,256]{2,0,1:T(2,128)S(1)}, u32[]{:S(2)}, u32[]{:S(2)}) %collective-permute-start) | collective-permute-done | bytes 526368 | tf_op jit(solution)/shard_map/ppermute | solution.py:19
  110.1 8.2 %collective-permute-done.1 = f32[2,257,256]{2,0,1:T(2,128)S(1)} collective-permute-done((f32[2,257,256]{2,0,1:T(2,128)S(1)}, f32[2,257,256]{2,0,1:T(2,128)S(1)}, u32[]{:S(2)}, u32[]{:S(2)}) %collective-permute-start.1) | collective-permute-done | bytes 526368 | tf_op jit(solution)/shard_map/ppermute | solution.py:21
  118.2 0.1 fusion.18
  118.3 0.9 slice.97
  119.3 0.2 copy.72
  119.5 1.5 reshape_squeeze.4
  121.1 0.6 fusion.19
  121.7 0.7 slice.98
  122.5 6.4 %psum.15 = f32[2,256]{1,0:T(2,128)S(1)} all-reduce(f32[2,256]{1,0:T(2,128)S(1)} %bitcast.109), channel_id=1, replica_groups=mesh['tm'=2,'space'=4,'member'=4] {'member'}, use_global_device_ids=true, to_apply=%region_4.5 | all-reduce | flops 512 | bytes 4096 | tf_op jit(solution)/shard_map/psum | solution.py:106
  128.8 23.1 %all-reduce.2.cloned.1.call-done = f32[2,256,256]{2,1,0:T(8,128)} async-done(((f32[2,256,256]{2,1,0:T(8,128)}), f32[2,256,256]{2,1,0:T(8,128)}) %all-reduce.2.cloned.1.call-update) | async-done | bytes 524304 | tf_op jit(solution)/shard_map/psum | solution.py:106
  151.9 2.1 %fusion.24 = f32[2,256,256]{1,2,0:T(8,128)S(1)} fusion(f32[2,256,256]{2,1,0:T(8,128)S(1)} %fusion.19, f32[2,256,256]{2,1,0:T(8,128)} %all-reduce.2.cloned.1.call-done, f32[256,256]{1,0:T(8,128)S(1)} %fusion.30), kind=kOutput, calls=%fused_computation.44 | convolution fusion | flops 402784256 | bytes 1835008 | tf_op jit(solution)/shard_map/tij,tjk->tik/dot_general | solution.py:113
  154.0 0.7 fusion.17
  154.7 1.1 fusion.43
  155.8 0.7 fusion.22
  156.5 1.1 fusion.15
  157.5 0.4 fusion.38
  157.9 0.4 fusion.36
  158.3 0.5 add_convert_fusion
  158.8 1.2 copy.116
  (46 shorter events, 0.9 us)
Async XLA Ops:
  19.4 4.4 %copy-start.4 = (s32[3,2,2,1024]{3,2,1,0:T(2,128)S(1)}, s32[3,2,2,1024]{3,2,1,0:T(2,128)}, u32[]{:S(2)}) copy-start(s32[3,2,2,1024]{3,2,1,0:T(2,128)} %param.21) | copy-start | bytes 147460
  19.4 4.4 %copy-start.5 = (bf16[3,2,2,1024]{3,2,1,0:T(2,128)(2,1)S(1)}, bf16[3,2,2,1024]{3,2,1,0:T(2,128)(2,1)}, u32[]{:S(2)}) copy-start(bf16[3,2,2,1024]{3,2,1,0:T(2,128)(2,1)} %param.20) | copy-start | bytes 73732
  19.4 4.4 %copy-start.6 = (bf16[3,2,2,1024]{3,2,1,0:T(2,128)(2,1)S(1)}, bf16[3,2,2,1024]{3,2,1,0:T(2,128)(2,1)}, u32[]{:S(2)}) copy-start(bf16[3,2,2,1024]{3,2,1,0:T(2,128)(2,1)} %param.19) | copy-start | bytes 73732
  19.4 24.4 %all-to-all-start = ((bf16[4,2,98304]{2,1,0:T(2,128)(2,1)}), bf16[4,2,98304]{2,1,0:T(2,128)(2,1)S(1)}, u32[]{:S(2)}, u32[]{:S(2)}) async-start(bf16[4,2,98304]{2,1,0:T(2,128)(2,1)} %reshape.154), calls=%async_computation | async-start | bytes 3145728 | tf_op jit(solution)/shard_map/all_to_all | solution.py:87
  60.6 3.9 %copy-start.8 = (s32[2,8]{1,0:T(2,128)S(1)}, s32[2,8]{1,0:T(2,128)}, u32[]{:S(2)}) copy-start(s32[2,8]{1,0:T(2,128)} %param.22) | copy-start | bytes 196
  60.6 23.7 %all-to-all-start.1 = ((bf16[3,2,2,259,256]{4,2,3,0,1:T(2,128)(2,1)}), bf16[3,2,2,259,256]{4,2,3,0,1:T(2,128)(2,1)S(1)}, u32[]{:S(2)}, u32[]{:S(2)}) async-start(bf16[3,2,2,259,256]{4,2,3,0,1:T(2,128)(2,1)} %pad_maximum_fusion), calls=%async_computation.1 | async-start | bytes 3182592 | tf_op jit(solution)/shard_map/all_to_all | solution.py:89
  64.4 87.5 %all-reduce.2.cloned.1.call-start = ((), (), s32[]{:S(2)}) async-start(), calls=%async_computation.2 | async-start | bytes 1048576 | tf_op jit(solution)/shard_map/psum | solution.py:106
  84.4 1.2 copy-start
  92.5 17.6 %collective-permute-start = (f32[2,257,256]{2,0,1:T(2,128)S(1)}, f32[2,257,256]{2,0,1:T(2,128)S(1)}, u32[]{:S(2)}, u32[]{:S(2)}) collective-permute-start(f32[2,257,256]{2,0,1:T(2,128)S(1)} %copy.79), channel_id=1, source_target_pairs={{0,4},{4,8},{8,12},{12,16},{16,20},{20,24},{24,28},{28,0},{1,5},{5... | collective-permute-start | bytes 1579016 | tf_op jit(solution)/shard_map/ppermute | solution.py:19
  94.6 24.7 %copy-start.1 = (f32[1,2,256,256]{3,2,1,0:T(8,128)S(1)}, f32[1,2,256,256]{3,2,1,0:T(8,128)}, u32[]{:S(2)}) copy-start(f32[1,2,256,256]{3,2,1,0:T(8,128)} %param.23) | copy-start | bytes 1572868
  94.6 23.6 %collective-permute-start.1 = (f32[2,257,256]{2,0,1:T(2,128)S(1)}, f32[2,257,256]{2,0,1:T(2,128)S(1)}, u32[]{:S(2)}, u32[]{:S(2)}) collective-permute-start(f32[2,257,256]{2,0,1:T(2,128)S(1)} %copy.81), channel_id=1, source_target_pairs={{4,0},{8,4},{12,8},{16,12},{20,16},{24,20},{28,24},{0,28},{5,1},{9... | collective-permute-start | bytes 1579016 | tf_op jit(solution)/shard_map/ppermute | solution.py:21
  118.3 1.0 copy-start.2
  119.3 1.7 %copy-start.7 = (f32[1,2,8,128]{3,2,1,0:T(8,128)S(1)}, f32[1,2,8,128]{3,2,1,0:T(8,128)}, u32[]{:S(2)}) copy-start(f32[1,2,8,128]{3,2,1,0:T(8,128)} %param.25) | copy-start | bytes 24580
  154.0 1.8 %copy-start.3 = (f32[2,256,256]{2,1,0:T(8,128)S(1)}, f32[2,256,256]{2,1,0:T(8,128)}, u32[]{:S(2)}) copy-start(f32[2,256,256]{2,1,0:T(8,128)} %all-reduce.2.cloned.1.call-done) | copy-start | bytes 1572868
Sparse Core Ops, SparseCore 0:
  119.4 32.4 all-reduce.1
where the time goes:
time: 168 us; the launch traced here: 167 us
  waiting for transfers between devices  83.2 us (50%)
  local copies, waits for them, and re-layouts  35.3 us (21%)
  between operations  13.7 us (8%)
  starting transfers between devices  13 us (8%)
  matrix products  10.8 us (6%)
  blocking collectives  6.37 us (4%)
  other arithmetic  4.26 us (3%)
    psum x1, waiting for transfers between devices, body(): gram_sums, proj_sums = lax.psum((gram_sums, proj_sums), 'member')  23.1 us
    unnamed x27, local copies, waits for them, and re-layouts  21.1 us
    all_to_all x1, waiting for transfers between devices, body(): lax.all_to_all(obs_anom, 'member', split_axis=4, concat_axis=3, tiled=True)  19.9 us
    all_to_all x1, waiting for transfers between devices, body(): lax.all_to_all(combined, 'tm', split_axis=1, concat_axis=0, tiled=True)  19.6 us
    ppermute x1, waiting for transfers between devices, with_halo(): lax.ppermute(tail, axis, [(i, (i + 1) % count) for i in range(count)])  12.5 us
    all_to_all x1, local copies, waits for them, and re-layouts, body(): lax.all_to_all(obs_anom, 'member', split_axis=4, concat_axis=3, tiled=True)  9.78 us
    ppermute x1, waiting for transfers between devices, with_halo(): lax.ppermute(head, axis, [((i + 1) % count, i) for i in range(count)])  8.16 us
    psum x1, blocking collectives, body(): gram_sums, proj_sums = lax.psum((gram_sums, proj_sums), 'member')  6.37 us
  transfers between devices with their start and end apart: 5, of which 5 were waited for; matrix products, arithmetic and copies ran while one was open for 2% of the time, Pallas kernels for 0%

commit v1 on v0

--- a/solution.py
+++ b/solution.py
@@ -84,7 +84,12 @@
     obs_info = jnp.stack([obs_prec, innov, placing], axis=3)
     quarter = obs_anom.shape[4] // lax.axis_size("member")
     own_part = lax.dynamic_slice_in_dim(obs_info, lax.axis_index("member") * quarter, quarter, 4)
-    ensemble = lax.all_to_all(obs_anom, "member", split_axis=4, concat_axis=3, tiled=True)
+    ensemble = jnp.concatenate(
+        lax.all_to_all(
+            jnp.stack(jnp.split(obs_anom, lax.axis_size("member"), axis=4)), "member", 0, 0
+        ),
+        axis=3,
+    )
     combined = jnp.concatenate([ensemble, own_part], axis=3)
     relaid = lax.all_to_all(combined, "tm", split_axis=1, concat_axis=0, tiled=True)[:, 0]
     tile_count = relaid.shape[1]

time: 168 us -> 143 us (0.85)
  local copies, waits for them, and re-layouts: 35.3 us -> 11.1 us
    unnamed x27 -> x23, local copies, waits for them, and re-layouts: 21.1 us -> 2.14 us
    all_to_all x1, local copies, waits for them, and re-layouts: 9.78 us -> 0.1 us  [body(): lax.all_to_all(jnp.stack(jnp.split(obs_anom, lax.axis_size('member'), axi...]
    concatenate x1, other arithmetic: 3.23 us -> 0.12 us  [body(): combined = jnp.concatenate([ensemble, own_part], axis=3)]
    concatenate x0 -> x1, local copies, waits for them, and re-layouts: none -> 2.37 us  [body(): combined = jnp.concatenate([ensemble, own_part], axis=3)]
where the time goes in v1:
time: 143 us; the launch traced here: 142 us
  waiting for transfers between devices  83.3 us (58%)
  starting transfers between devices  14 us (10%)
  between operations  13.7 us (10%)
  local copies, waits for them, and re-layouts  11.1 us (8%)
  matrix products  10.8 us (8%)
  blocking collectives  6.81 us (5%)
  other arithmetic  2.6 us (2%)
    psum x1, waiting for transfers between devices, body(): gram_sums, proj_sums = lax.psum((gram_sums, proj_sums), 'member')  23.2 us
    all_to_all x1, waiting for transfers between devices, body(): lax.all_to_all(jnp.stack(jnp.split(obs_anom, lax.axis_size('member'), axi...  19.7 us
    all_to_all x1, waiting for transfers between devices, body(): lax.all_to_all(combined, 'tm', split_axis=1, concat_axis=0, tiled=True)  19.7 us
    ppermute x1, waiting for transfers between devices, with_halo(): lax.ppermute(tail, axis, [(i, (i + 1) % count) for i in range(count)])  12.5 us
    ppermute x1, waiting for transfers between devices, with_halo(): lax.ppermute(head, axis, [((i + 1) % count, i) for i in range(count)])  8.13 us
    psum x1, blocking collectives, body(): gram_sums, proj_sums = lax.psum((gram_sums, proj_sums), 'member')  6.81 us
    all_to_all x1, starting transfers between devices, body(): lax.all_to_all(combined, 'tm', split_axis=1, concat_axis=0, tiled=True)  4.77 us
    all_to_all x1, starting transfers between devices, body(): lax.all_to_all(jnp.stack(jnp.split(obs_anom, lax.axis_size('member'), axi...  4.37 us
  transfers between devices with their start and end apart: 5, of which 5 were waited for; matrix products, arithmetic and copies ran while one was open for 2% of the time, Pallas kernels for 0%

profile of v1, /device:TPU:0, one launch (start us, length us, event | category | flops | bytes accessed | tf_op | source)
XLA Modules:
  0.0 142.5 jit_solution(11233062176115798018)
XLA Ops:
  6.5 1.5 %slice_bitcast_fusion.3 = (bf16[1,3,2,2,64,256]{5,4,3,2,1,0:T(8,128)(2,1)S(1)}, bf16[1,3,2,2,64,256]{5,4,3,2,1,0:T(8,128)(2,1)S(1)}, bf16[1,3,2,2,64,256]{5,4,3,...) fusion(bf16[3,2,2,64,1024]{4,3,2,1,0:T(8,128)(2,1)} %param.18), kind=kLoop, calls=%fused_computation.50 | loop fusion | bytes 3145728 | tf_op jit(solution)/shard_map/stack | solution.py:89
  8.0 1.4 pad_maximum_fusion.1
  9.4 4.4 %all-to-all-start = ((bf16[4,3,2,2,64,256]{5,4,3,2,1,0:T(8,128)(2,1)}), bf16[4,3,2,2,64,256]{5,4,3,2,1,0:T(8,128)(2,1)S(1)}, u32[]{:S(2)}, u32[]{:S(2)}) async-start(bf16[4,3,2,2,64,256]{5,4,3,2,1,0:T(8,128)(2,1)} %pad_maximum_fusion.1), calls=%async_computation | async-start | bytes 3145728 | tf_op jit(solution)/shard_map/all_to_all | solution.py:88
  13.9 0.1 fusion.32
  14.1 19.7 %all-to-all-done = bf16[4,3,2,2,64,256]{5,4,3,2,1,0:T(8,128)(2,1)S(1)} async-done(((bf16[4,3,2,2,64,256]{5,4,3,2,1,0:T(8,128)(2,1)}), bf16[4,3,2,2,64,256]{5,4,3,2,1,0:T(8,128)(2,1)S(1)}, u32[]{:S(2)}, u32[]{:S(2)}) %all-to-all-start) | async-done | bytes 1572896 | tf_op jit(solution)/shard_map/all_to_all | solution.py:88
  33.8 0.1 copy.85
  33.9 0.1 pad_maximum_fusion
  34.0 2.4 %copy.89 = bf16[3,2,2,259,256]{4,2,3,0,1:T(2,128)(2,1)} copy(bf16[3,2,2,259,256]{4,3,2,1,0:T(8,128)(2,1)S(1)} %pad_maximum_fusion) | data formatting | bytes 3182592 | tf_op jit(solution)/shard_map/concatenate | solution.py:93
  36.4 4.8 %all-to-all-start.1 = ((bf16[3,2,2,259,256]{4,2,3,0,1:T(2,128)(2,1)}), bf16[3,2,2,259,256]{4,2,3,0,1:T(2,128)(2,1)}, u32[]{:S(2)}, u32[]{:S(2)}) async-start(bf16[3,2,2,259,256]{4,2,3,0,1:T(2,128)(2,1)} %copy.89), calls=%async_computation.1 | async-start | bytes 3182592 | tf_op jit(solution)/shard_map/all_to_all | solution.py:94
  41.3 0.2 select_reduce_fusion
  41.5 19.7 %all-to-all-done.1 = bf16[3,2,2,259,256]{4,2,3,0,1:T(2,128)(2,1)} async-done(((bf16[3,2,2,259,256]{4,2,3,0,1:T(2,128)(2,1)}), bf16[3,2,2,259,256]{4,2,3,0,1:T(2,128)(2,1)}, u32[]{:S(2)}, u32[]{:S(2)}) %all-to-all-start.1) | async-done | bytes 1591328 | tf_op jit(solution)/shard_map/all_to_all | solution.py:94
  61.2 1.6 %copy.118 = bf16[3,2,2,259,256]{4,3,0,1,2:T(8,128)(2,1)S(1)} copy(bf16[3,2,2,259,256]{4,2,3,0,1:T(2,128)(2,1)} %all-to-all-done.1) | data formatting | bytes 3182592 | tf_op jit(solution)/shard_map/squeeze | solution.py:94
  62.9 0.1 broadcast_in_dim.48
  63.0 4.5 %while.20 = (s32[]{:T(128)}, f32[6,256,256]{2,1,0:T(8,128)S(1)}, f32[6,256]{1,0:T(8,128)S(1)}, bf16[6,2,259,256]{3,2,0,1:T(8,128)(2,1)S(1)}, f32[6]{0:T(128)S(1)}, /*index=5*/s32[]{:T(128)}, s32[]{:T(128)}) while((s32[]{:T(128)}, f32[6,256,256]{2,1,0:T(8,128)S(1)}, f32[6,256]{1,0:T(8,128)S(1)}, ...), condition=%wide.region_2.3_spmd.clone, body=%wide.region_1.2_spmd.clone.sunk | while | flops 1015346944 | bytes 9977029 | solution.py:78
  63.2 0.1 multiply_multiply_fusion.3
  63.3 0.1 slice_convert_fusion.7
  63.5 1.4 fusion.58
  64.8 0.3 fusion.59
  65.5 0.1 multiply_multiply_fusion.3
  65.6 0.1 slice_convert_fusion.7
  65.7 1.4 fusion.58
  67.1 0.3 fusion.59
  67.5 0.1 constant_dynamic-update-slice_fusion
  67.8 0.1 fusion.40
  67.9 0.3 copy.92
  68.1 1.8 %collective-permute-start = (f32[2,257,256]{2,0,1:T(2,128)S(1)}, f32[2,257,256]{2,0,1:T(2,128)S(1)}, u32[]{:S(2)}, u32[]{:S(2)}) collective-permute-start(f32[2,257,256]{2,0,1:T(2,128)S(1)} %copy.92), channel_id=1, source_target_pairs={{0,4},{4,8},{8,12},{12,16},{16,20},{20,24},{24,28},{28,0},{1,5},{5... | collective-permute-start | bytes 1579016 | tf_op jit(solution)/shard_map/ppermute | solution.py:19
  70.0 0.3 copy.94
  70.3 3.0 %collective-permute-start.1 = (f32[2,257,256]{2,0,1:T(2,128)S(1)}, f32[2,257,256]{2,0,1:T(2,128)S(1)}, u32[]{:S(2)}, u32[]{:S(2)}) collective-permute-start(f32[2,257,256]{2,0,1:T(2,128)S(1)} %copy.94), channel_id=1, source_target_pairs={{4,0},{8,4},{12,8},{16,12},{20,16},{24,20},{28,24},{0,28},{5,1},{9... | collective-permute-start | bytes 1579016 | tf_op jit(solution)/shard_map/ppermute | solution.py:21
  73.3 12.5 %collective-permute-done = f32[2,257,256]{2,0,1:T(2,128)S(1)} collective-permute-done((f32[2,257,256]{2,0,1:T(2,128)S(1)}, f32[2,257,256]{2,0,1:T(2,128)S(1)}, u32[]{:S(2)}, u32[]{:S(2)}) %collective-permute-start) | collective-permute-done | bytes 526368 | tf_op jit(solution)/shard_map/ppermute | solution.py:19
  85.7 8.1 %collective-permute-done.1 = f32[2,257,256]{2,0,1:T(2,128)S(1)} collective-permute-done((f32[2,257,256]{2,0,1:T(2,128)S(1)}, f32[2,257,256]{2,0,1:T(2,128)S(1)}, u32[]{:S(2)}, u32[]{:S(2)}) %collective-permute-start.1) | collective-permute-done | bytes 526368 | tf_op jit(solution)/shard_map/ppermute | solution.py:21
  93.9 0.1 fusion.18
  94.0 0.8 slice.97
  95.0 0.2 copy.84
  95.2 0.4 copy-done.3
  95.6 0.5 reshape_squeeze.4
  96.1 0.6 fusion.19
  96.8 0.7 slice.98
  97.5 6.8 %psum.15 = f32[2,256]{1,0:T(2,128)S(1)} all-reduce(f32[2,256]{1,0:T(2,128)S(1)} %bitcast.111), channel_id=1, replica_groups=mesh['tm'=2,'space'=4,'member'=4] {'member'}, use_global_device_ids=true, to_apply=%region_4.5 | all-reduce | flops 512 | bytes 4096 | tf_op jit(solution)/shard_map/psum | solution.py:111
  104.3 23.2 %all-reduce.2.cloned.1.call-done = f32[2,256,256]{2,1,0:T(8,128)} async-done(((f32[2,256,256]{2,1,0:T(8,128)}), f32[2,256,256]{2,1,0:T(8,128)}) %all-reduce.2.cloned.1.call-update) | async-done | bytes 524304 | tf_op jit(solution)/shard_map/psum | solution.py:111
  127.5 2.1 %fusion.24 = f32[2,256,256]{1,2,0:T(8,128)S(1)} fusion(f32[2,256,256]{2,1,0:T(8,128)S(1)} %fusion.19, f32[2,256,256]{2,1,0:T(8,128)} %all-reduce.2.cloned.1.call-done, f32[256,256]{1,0:T(8,128)S(1)} %fusion.30), kind=kOutput, calls=%fused_computation.45 | convolution fusion | flops 402784256 | bytes 1835008 | tf_op jit(solution)/shard_map/tij,tjk->tik/dot_general | solution.py:118
  129.6 0.7 fusion.17
  130.3 1.1 fusion.41
  131.4 0.7 fusion.22
  132.1 1.1 fusion.15
  133.1 0.4 fusion.36
  133.5 0.4 fusion.34
  133.9 0.5 add_convert_fusion
  134.4 1.2 copy.130
  (48 shorter events, 1.0 us)
Async XLA Ops:
  9.4 4.4 %copy-start.4 = (s32[3,2,2,1024]{3,2,1,0:T(2,128)S(1)}, s32[3,2,2,1024]{3,2,1,0:T(2,128)}, u32[]{:S(2)}) copy-start(s32[3,2,2,1024]{3,2,1,0:T(2,128)} %param.21) | copy-start | bytes 147460
  9.4 4.5 %copy-start.5 = (bf16[3,2,2,1024]{3,2,1,0:T(2,128)(2,1)S(1)}, bf16[3,2,2,1024]{3,2,1,0:T(2,128)(2,1)}, u32[]{:S(2)}) copy-start(bf16[3,2,2,1024]{3,2,1,0:T(2,128)(2,1)} %param.19) | copy-start | bytes 73732
  9.4 4.5 %copy-start.6 = (bf16[3,2,2,1024]{3,2,1,0:T(2,128)(2,1)S(1)}, bf16[3,2,2,1024]{3,2,1,0:T(2,128)(2,1)}, u32[]{:S(2)}) copy-start(bf16[3,2,2,1024]{3,2,1,0:T(2,128)(2,1)} %param.20) | copy-start | bytes 73732
  9.4 24.4 %all-to-all-start = ((bf16[4,3,2,2,64,256]{5,4,3,2,1,0:T(8,128)(2,1)}), bf16[4,3,2,2,64,256]{5,4,3,2,1,0:T(8,128)(2,1)S(1)}, u32[]{:S(2)}, u32[]{:S(2)}) async-start(bf16[4,3,2,2,64,256]{5,4,3,2,1,0:T(8,128)(2,1)} %pad_maximum_fusion.1), calls=%async_computation | async-start | bytes 3145728 | tf_op jit(solution)/shard_map/all_to_all | solution.py:88
  36.4 4.8 %copy-start.8 = (s32[2,8]{1,0:T(2,128)S(1)}, s32[2,8]{1,0:T(2,128)}, u32[]{:S(2)}) copy-start(s32[2,8]{1,0:T(2,128)} %param.22) | copy-start | bytes 196
  36.4 24.8 %all-to-all-start.1 = ((bf16[3,2,2,259,256]{4,2,3,0,1:T(2,128)(2,1)}), bf16[3,2,2,259,256]{4,2,3,0,1:T(2,128)(2,1)}, u32[]{:S(2)}, u32[]{:S(2)}) async-start(bf16[3,2,2,259,256]{4,2,3,0,1:T(2,128)(2,1)} %copy.89), calls=%async_computation.1 | async-start | bytes 3182592 | tf_op jit(solution)/shard_map/all_to_all | solution.py:94
  41.2 86.3 %all-reduce.2.cloned.1.call-start = ((), (), s32[]{:S(2)}) async-start(), calls=%async_computation.2 | async-start | bytes 1048576 | tf_op jit(solution)/shard_map/psum | solution.py:111
  68.1 17.6 %collective-permute-start = (f32[2,257,256]{2,0,1:T(2,128)S(1)}, f32[2,257,256]{2,0,1:T(2,128)S(1)}, u32[]{:S(2)}, u32[]{:S(2)}) collective-permute-start(f32[2,257,256]{2,0,1:T(2,128)S(1)} %copy.92), channel_id=1, source_target_pairs={{0,4},{4,8},{8,12},{12,16},{16,20},{20,24},{24,28},{28,0},{1,5},{5... | collective-permute-start | bytes 1579016 | tf_op jit(solution)/shard_map/ppermute | solution.py:19
  70.3 24.7 %copy-start = (f32[1,2,256,256]{3,2,1,0:T(8,128)S(1)}, f32[1,2,256,256]{3,2,1,0:T(8,128)}, u32[]{:S(2)}) copy-start(f32[1,2,256,256]{3,2,1,0:T(8,128)} %param.23) | copy-start | bytes 1572868
  70.3 23.6 %collective-permute-start.1 = (f32[2,257,256]{2,0,1:T(2,128)S(1)}, f32[2,257,256]{2,0,1:T(2,128)S(1)}, u32[]{:S(2)}, u32[]{:S(2)}) collective-permute-start(f32[2,257,256]{2,0,1:T(2,128)S(1)} %copy.94), channel_id=1, source_target_pairs={{4,0},{8,4},{12,8},{16,12},{20,16},{24,20},{28,24},{0,28},{5,1},{9... | collective-permute-start | bytes 1579016 | tf_op jit(solution)/shard_map/ppermute | solution.py:21
  94.0 1.0 copy-start.1
  94.0 1.6 %copy-start.3 = (bf16[1,2,256,8,128]{4,3,2,1,0:T(8,128)(2,1)S(1)}, bf16[1,2,256,8,128]{4,3,2,1,0:T(8,128)(2,1)}, u32[]{:S(2)}) copy-start(bf16[1,2,256,8,128]{4,3,2,1,0:T(8,128)(2,1)} %param.24) | copy-start | bytes 3145732
  95.0 1.1 copy-start.7
  129.6 1.8 %copy-start.2 = (f32[2,256,256]{2,1,0:T(8,128)S(1)}, f32[2,256,256]{2,1,0:T(8,128)}, u32[]{:S(2)}) copy-start(f32[2,256,256]{2,1,0:T(8,128)} %all-reduce.2.cloned.1.call-done) | copy-start | bytes 1572868
Sparse Core Ops, SparseCore 0:
  95.0 32.4 all-reduce.1
